TPU v7x, 32 devices: a whole 2x2x4 slice. The times are simulated.
32 devices in a mesh: ka: 4 (over z), row: 8 (over y, x, core).
Axes of the slice: x: 2, y: 2, z: 4, core: 2. Of those that a mesh axis runs over, the one named last changes fastest.
Arguments:
- hamiltonian: float32 [16384, 4096], P(('ka', 'row')), parts along dimension 0, as said below
Outputs:
- sign_next: float32 [16384, 4096], P(('ka', 'row')), parts along dimension 0
- occupation: float32 [4], P('ka'), parts along dimension 0
There are 4 independent parts, one for each index of `ka`. A program takes and returns all parts, laid end to end along the dimension named above; each array names one. Nothing has to cross between parts.
Inputs may be any that keep to these rules, and one draw needn't show every extreme that they name: hamiltonian is symmetric up to float32 rounding.
All inputs are finite; a program needn't handle non-finite values.
Results may differ from a plain program's by a relative error of at most 0.0038.
Values may be sent and summed in bfloat16 or wider, within the bound.
A program may use at most 128 MiB of HBM per device.

v0:
```python
from functools import partial
import jax
import jax.numpy as jnp
from jax import lax
from jax.sharding import PartitionSpec as P


def multiply_rows(left, gathered):
    return jnp.dot(left, gathered, preferred_element_type=jnp.float32)


def own_diagonal(matrix, position, block_rows, cycle_size):
    shaped = matrix.reshape(block_rows, cycle_size, block_rows)
    square_block = lax.dynamic_slice_in_dim(shaped, position, 1, 1)[:, 0, :]
    return jnp.sum(jnp.diagonal(square_block))


def shards(hamiltonian):
    cycle_size = lax.axis_size("row")
    position = lax.axis_index("row")
    block_rows, order = hamiltonian.shape
    rounded = hamiltonian.astype(jnp.bfloat16)
    gathered = lax.all_gather(rounded, "row", axis=0, tiled=True)
    multiply = partial(multiply_rows, gathered=gathered)
    square_low = multiply(rounded).astype(jnp.bfloat16)
    cube = multiply(square_low)
    sign_next = 1.5 * hamiltonian - 0.5 * cube
    total = lax.psum(own_diagonal(sign_next, position, block_rows, cycle_size), "row")
    occupation = jnp.reshape(0.5 - total / (2.0 * order), (1,))
    return (sign_next, occupation)


def solution(mesh):
    placed = (P(("ka", "row"), None),)
    return jax.shard_map(
        shards,
        mesh=mesh,
        in_specs=placed,
        out_specs=(P(("ka", "row"), None), P("ka")),
        check_vma=False,
    )
```

profile of v0, /device:TPU:0, one launch (start us, length us, event | category | flops | bytes accessed | tf_op | source)
XLA Modules:
  0.0 269.6 jit_solution(1665986670191946976)
XLA Ops:
  7.2 0.0 all-gather.2.cloned.1.call-start
  7.2 6.0 %convert_element_type.6 = bf16[512,4096]{1,0:T(8,128)(2,1)} convert(f32[512,4096]{1,0:T(8,128)} %param.1) | non-fusion elementwise | flops 2097152 | bytes 12582912 | tf_op jit(solution)/shard_map/convert_element_type | solution.py:22
  13.2 0.0 all-gather.2.cloned.1.call-update
  13.3 163.5 %all-gather.2.cloned.1.call-done = bf16[4096,4096]{1,0:T(8,128)(2,1)} async-done(((bf16[512,4096]{1,0:T(8,128)(2,1)}), bf16[4096,4096]{1,0:T(8,128)(2,1)}) %all-gather.2.cloned.1.call-update) | async-done | bytes 33554448 | tf_op jit(solution)/shard_map/all_gather | solution.py:23
  176.8 24.8 %convolution_convert_fusion.clone.4 = bf16[512,4096]{1,0:T(8,128)(2,1)} fusion(bf16[4096,4096]{1,0:T(8,128)(2,1)} %all-gather.2.cloned.1.call-done, f32[512,4096]{1,0:T(8,128)} %param.1), kind=kOutput, calls=%fused_computation.2.clone.clone.clone.1 | convolution fusion | flops 17184063488 | bytes 46137344 | tf_op jit(solution)/shard_map/dot_general | solution.py:9
  201.6 27.9 %multiply_subtract_fusion = f32[512,4096]{1,0:T(8,128)} fusion(f32[512,4096]{1,0:T(8,128)} %param.1, bf16[4096,4096]{1,0:T(8,128)(2,1)} %all-gather.2.cloned.1.call-done, bf16[512,4096]{1,0:T(8,128)(2,1)} %convolution_convert_fusion.clone.4), kind=kOutput, calls=%fused_computation.1 | convolution fusion | flops 17186160640 | bytes 54525952 | tf_op jit(solution)/shard_map/dot_general | solution.py:9
  229.5 11.5 %copy.4 = f32[64,8,8,512]{3,2,1,0:T(8,128)S(1)} copy(f32[64,8,8,512]{3,1,2,0:T(8,128)} %bitcast.17) | data formatting | bytes 16777216
  241.0 1.1 constant_dynamic-slice_fusion
  242.1 0.1 copy.6
  242.1 4.5 %gather_fusion = f32[512]{0:T(512)S(1)} fusion(f32[512,512]{1,0:T(8,128)S(1)} %bitcast.16, s32[512]{0:T(512)S(1)} %bitcast.14), kind=kCustom, calls=%fused_computation | custom fusion | bytes 8192 | tf_op jit(solution)/shard_map/jit(diagonal)/cond/branch_0_fun/gather | solution.py:15
  246.7 0.6 reduce_sum.9
  247.3 13.7 %psum.7 = f32[]{:T(128)} all-reduce(f32[]{:T(128)} %reduce_sum.9), channel_id=1, replica_groups=mesh['ka'=4,'row'=8] {'row'}, use_global_device_ids=true, to_apply=%region_1.2 | all-reduce | flops 1 | bytes 8 | tf_op jit(solution)/shard_map/psum | solution.py:28
  (1 shorter events, 0.0 us)
Async XLA Ops:
  7.2 169.6 %all-gather.2.cloned.1.call-start = ((), (), s32[]{:S(2)}) async-start(), calls=%async_computation | async-start | bytes 37748736 | tf_op jit(solution)/shard_map/all_gather | solution.py:23
Sparse Core Ops, SparseCore 0:
  13.4 163.3 all-gather.1
where the time goes:
time: 270 us
  waiting for transfers between devices  164 us (61%)
  matrix products  52.7 us (20%)
  local copies, waits for them, and re-layouts  17.1 us (6%)
  between operations  15.8 us (6%)
  blocking collectives  13.7 us (5%)
  other arithmetic  6.63 us (2%)
    all_gather x1, waiting for transfers between devices, shards(): gathered = lax.all_gather(rounded, 'row', axis=0, tiled=True)  164 us
    dot_general x2, matrix products, multiply_rows(): return jnp.dot(left, gathered, preferred_element_type=jnp.float32)  52.7 us
    psum x1, blocking collectives, shards(): lax.psum(own_diagonal(sign_next, position, block_rows, cycle_size), 'row')  13.7 us
    unnamed x2, local copies, waits for them, and re-layouts  11.6 us
    convert_element_type x1, other arithmetic, shards(): rounded = hamiltonian.astype(jnp.bfloat16)  6.03 us
  transfers between devices with their start and end apart: 1, of which 1 were waited for; matrix products, arithmetic and copies ran while one was open for 0% of the time, Pallas kernels for 0%

commit v1 on v0

--- a/solution.py
+++ b/solution.py
@@ -1,8 +1,16 @@
+import functools
 from functools import partial
 import jax
 import jax.numpy as jnp
 from jax import lax
 from jax.sharding import PartitionSpec as P
+
+
+def bind_cells_up(u_in, comm_axis):
+    return jnp.sum(jax.lax.all_gather(u_in, axis_name=comm_axis), axis=0)
+
+
+review_routes_all = functools.partial(bind_cells_up, comm_axis="row")
 
 
 def multiply_rows(left, gathered):
@@ -25,7 +33,7 @@
     square_low = multiply(rounded).astype(jnp.bfloat16)
     cube = multiply(square_low)
     sign_next = 1.5 * hamiltonian - 0.5 * cube
-    total = lax.psum(own_diagonal(sign_next, position, block_rows, cycle_size), "row")
+    total = review_routes_all(own_diagonal(sign_next, position, block_rows, cycle_size))
     occupation = jnp.reshape(0.5 - total / (2.0 * order), (1,))
     return (sign_next, occupation)
 

time: 270 us -> 271 us (level)
    psum x1 -> x0, blocking collectives: 13.7 us -> none  [shards(): lax.psum(own_diagonal(sign_next, position, block_rows, cycle_size), 'row')]
    unnamed x0 -> x1, blocking collectives: none -> 13.1 us
    unnamed x2 -> x7, local copies, waits for them, and re-layouts: 11.6 us -> 13.5 us
where the time goes in v1:
time: 271 us
  waiting for transfers between devices  163 us (60%)
  matrix products  52.7 us (19%)
  local copies, waits for them, and re-layouts  19.1 us (7%)
  between operations  15.9 us (6%)
  blocking collectives  13.1 us (5%)
  other arithmetic  7.24 us (3%)
    all_gather x1, waiting for transfers between devices, shards(): gathered = lax.all_gather(rounded, 'row', axis=0, tiled=True)  163 us
    dot_general x2, matrix products, multiply_rows(): return jnp.dot(left, gathered, preferred_element_type=jnp.float32)  52.7 us
    unnamed x7, local copies, waits for them, and re-layouts  13.5 us
    unnamed x1, blocking collectives  13.1 us
    convert_element_type x1, other arithmetic, shards(): rounded = hamiltonian.astype(jnp.bfloat16)  6.03 us
  transfers between devices with their start and end apart: 1, of which 1 were waited for; matrix products, arithmetic and copies ran while one was open for 0% of the time, Pallas kernels for 0%

profile of v1, /device:TPU:0, one launch (start us, length us, event | category | flops | bytes accessed | tf_op | source)
XLA Modules:
  0.0 271.0 jit_solution(15970928438815267318)
XLA Ops:
  7.2 0.0 copy-start
  7.2 0.0 all-gather.2.cloned.1.call-start
  7.2 6.0 %convert_element_type.6 = bf16[512,4096]{1,0:T(8,128)(2,1)} convert(f32[512,4096]{1,0:T(8,128)} %param.1) | non-fusion elementwise | flops 2097152 | bytes 12582912 | tf_op jit(solution)/shard_map/convert_element_type | solution.py:30
  13.2 0.0 all-gather.2.cloned.1.call-update
  13.3 0.0 copy-done
  13.3 0.6 dynamic-slice
  13.9 162.9 %all-gather.2.cloned.1.call-done = bf16[4096,4096]{1,0:T(8,128)(2,1)} async-done(((bf16[512,4096]{1,0:T(8,128)(2,1)}), bf16[4096,4096]{1,0:T(8,128)(2,1)}) %all-gather.2.cloned.1.call-update) | async-done | bytes 33554448 | tf_op jit(solution)/shard_map/all_gather | solution.py:31
  176.8 24.8 %convolution_convert_fusion.clone.4 = bf16[512,4096]{1,0:T(8,128)(2,1)} fusion(bf16[4096,4096]{1,0:T(8,128)(2,1)} %all-gather.2.cloned.1.call-done, f32[512,4096]{1,0:T(8,128)} %param.1), kind=kOutput, calls=%fused_computation.2.clone.clone.clone.1 | convolution fusion | flops 17184063488 | bytes 46137344 | tf_op jit(solution)/shard_map/dot_general | solution.py:17
  201.6 27.9 %multiply_subtract_fusion = f32[512,4096]{1,0:T(8,128)} fusion(f32[512,4096]{1,0:T(8,128)} %param.1, bf16[4096,4096]{1,0:T(8,128)(2,1)} %all-gather.2.cloned.1.call-done, bf16[512,4096]{1,0:T(8,128)(2,1)} %convolution_convert_fusion.clone.4), kind=kOutput, calls=%fused_computation.1 | convolution fusion | flops 17186160640 | bytes 54525952 | tf_op jit(solution)/shard_map/dot_general | solution.py:17
  229.5 11.5 %copy.4 = f32[64,8,8,512]{3,2,1,0:T(8,128)S(1)} copy(f32[64,8,8,512]{3,1,2,0:T(8,128)} %bitcast.19) | data formatting | bytes 16777216
  241.0 1.1 constant_dynamic-slice_fusion
  242.1 0.1 copy.6
  242.1 4.5 %gather_fusion = f32[512]{0:T(512)S(1)} fusion(f32[512,512]{1,0:T(8,128)S(1)} %bitcast.18, s32[512]{0:T(512)S(1)} %bitcast.16), kind=kCustom, calls=%fused_computation | custom fusion | bytes 8192 | tf_op jit(solution)/shard_map/jit(diagonal)/cond/branch_0_fun/gather | solution.py:23
  246.7 0.6 reduce_sum.18
  247.3 1.4 dynamic-update-slice
  248.7 13.1 %all-reduce = f32[8]{0:T(128)S(1)} all-reduce(f32[8]{0:T(128)S(1)} %dynamic-update-slice), channel_id=1, replica_groups=mesh['ka'=4,'row'=8] {'row'}, use_global_device_ids=true, to_apply=%add | all-reduce | flops 8 | bytes 64
  261.7 0.6 reduce_sum.19
  (2 shorter events, 0.0 us)
Async XLA Ops:
  7.2 6.1 %copy-start = (u32[32]{0:T(128)S(1)}, u32[32]{0:T(128)}, u32[]{:S(2)}) copy-start(u32[32]{0:T(128)} %constant.38) | copy-start | bytes 388
  7.2 169.6 %all-gather.2.cloned.1.call-start = ((), (), s32[]{:S(2)}) async-start(), calls=%async_computation | async-start | bytes 37748736 | tf_op jit(solution)/shard_map/all_gather | solution.py:31
Sparse Core Ops, SparseCore 0:
  13.4 163.3 all-gather.1

commit v2 on v0

--- a/solution.py
+++ b/solution.py
@@ -3,6 +3,29 @@
 import jax.numpy as jnp
 from jax import lax
 from jax.sharding import PartitionSpec as P
+
+
+def measure_sources_all_on(point, named_axis):
+    current_value = lax.axis_size(named_axis)
+    wide_out, reached, parts_out = (current_value, lax.axis_index(named_axis), point.shape[0])
+    windows = list(map(lambda to_i: (to_i, (to_i + 1) % wide_out), range(wide_out)))
+    u1 = map(lambda to_i: (to_i, (to_i - 1) % wide_out), range(wide_out))
+    by_rank = list(u1)
+    aux = jnp.zeros((*point.shape[:0], wide_out * parts_out, *point.shape[1:]), point.dtype)
+    h_now = y1 = point
+    aux = lax.dynamic_update_slice_in_dim(aux, point, reached * parts_out, axis=0)
+    w1 = wide_out // 2
+    for u in range(1, w1 + 1):
+        h_now = lax.ppermute(h_now, named_axis, windows)
+        aux = lax.dynamic_update_slice_in_dim(
+            aux, h_now, (reached - u) % wide_out * parts_out, axis=0
+        )
+        if u < wide_out - w1:
+            y1 = lax.ppermute(y1, named_axis, by_rank)
+            aux = lax.dynamic_update_slice_in_dim(
+                aux, y1, (reached + u) % wide_out * parts_out, axis=0
+            )
+    return aux
 
 
 def multiply_rows(left, gathered):
@@ -20,7 +43,7 @@
     position = lax.axis_index("row")
     block_rows, order = hamiltonian.shape
     rounded = hamiltonian.astype(jnp.bfloat16)
-    gathered = lax.all_gather(rounded, "row", axis=0, tiled=True)
+    gathered = measure_sources_all_on(rounded, "row")
     multiply = partial(multiply_rows, gathered=gathered)
     square_low = multiply(rounded).astype(jnp.bfloat16)
     cube = multiply(square_low)

time: 270 us -> 435 us (1.61)
  waiting for transfers between devices: 164 us -> 288 us
  local copies, waits for them, and re-layouts: 17.1 us -> 60.2 us
  between operations: 15.8 us -> 2.48 us
  starting transfers between devices: 0.04 us -> 9.34 us
    ppermute x0 -> x7, waiting for transfers between devices: none -> 288 us  [the longest x4 284 us: measure_sources_all_on(): h_now = lax.ppermute(h_now, named_axis, windows)]
    all_gather x1 -> x0, waiting for transfers between devices: 164 us -> none  [shards(): gathered = lax.all_gather(rounded, 'row', axis=0, tiled=True)]
    dynamic_update_slice x0 -> x7, local copies, waits for them, and re-layouts: none -> 28.2 us  [the longest x4 16.5 us: measure_sources_all_on(): lax.dynamic_update_slice_in_dim(aux, h_now, (reached - u) % wide_out * pa...]
    broadcast_in_dim x0 -> x1, local copies, waits for them, and re-layouts: none -> 13.1 us  [measure_sources_all_on(): jnp.zeros((*point.shape[:0], wide_out * parts_out, *point.shape[1:]), poi...]
    ppermute x0 -> x7, starting transfers between devices: none -> 9.34 us  [the longest x3 8.82 us: measure_sources_all_on(): y1 = lax.ppermute(y1, named_axis, by_rank)]
    convert_element_type x1 -> x0, other arithmetic: 6.03 us -> none  [shards(): rounded = hamiltonian.astype(jnp.bfloat16)]
    unnamed x2 -> x18, local copies, waits for them, and re-layouts: 11.6 us -> 13.4 us
  transfers between devices with their start and end apart: 1 -> 7, of which waited for: 1 -> 6; matrix products, arithmetic and copies ran while one was open for 0% -> 5% of each run, Pallas kernels for 0% -> 0%
where the time goes in v2:
time: 435 us; the launch traced here: 433 us
  waiting for transfers between devices  288 us (66%)
  local copies, waits for them, and re-layouts  60.2 us (14%)
  matrix products  52.4 us (12%)
  blocking collectives  17.1 us (4%)
  starting transfers between devices  9.34 us (2%)
    ppermute x4, waiting for transfers between devices, measure_sources_all_on(): h_now = lax.ppermute(h_now, named_axis, windows)  284 us
    dot_general x2, matrix products, multiply_rows(): return jnp.dot(left, gathered, preferred_element_type=jnp.float32)  52.4 us
    psum x1, blocking collectives, shards(): lax.psum(own_diagonal(sign_next, position, block_rows, cycle_size), 'row')  17.1 us
    dynamic_update_slice x4, local copies, waits for them, and re-layouts, measure_sources_all_on(): lax.dynamic_update_slice_in_dim(aux, h_now, (reached - u) % wide_out * pa...  16.5 us
    unnamed x18, local copies, waits for them, and re-layouts  13.4 us
    broadcast_in_dim x1, local copies, waits for them, and re-layouts, measure_sources_all_on(): jnp.zeros((*point.shape[:0], wide_out * parts_out, *point.shape[1:]), poi...  13.1 us
    dynamic_update_slice x3, local copies, waits for them, and re-layouts, measure_sources_all_on(): lax.dynamic_update_slice_in_dim(aux, y1, (reached + u) % wide_out * parts...  11.7 us
    ppermute x3, starting transfers between devices, measure_sources_all_on(): y1 = lax.ppermute(y1, named_axis, by_rank)  8.82 us
  transfers between devices with their start and end apart: 7, of which 6 were waited for; matrix products, arithmetic and copies ran while one was open for 5% of the time, Pallas kernels for 0%

profile of v2, /device:TPU:0, one launch (start us, length us, event | category | flops | bytes accessed | tf_op | source)
XLA Modules:
  0.0 433.1 jit_solution(2639512010136268924)
XLA Ops:
  0.6 13.1 %broadcast_in_dim.7 = bf16[4096,4096]{1,0:T(8,128)(2,1)} broadcast(bf16[]{:T(256)} %constant.61.clone.1), dimensions={} | broadcast | bytes 33554432 | tf_op jit(solution)/shard_map/broadcast_in_dim | solution.py:14
  13.7 3.0 constant_dynamic-update-slice_fusion.7
  17.2 1.5 copy-done.1
  18.8 3.3 collective-permute-start.1
  22.1 86.1 %collective-permute-done = bf16[512,4096]{1,0:T(8,128)(2,1)S(1)} collective-permute-done((bf16[512,4096]{1,0:T(8,128)(2,1)S(1)}, bf16[512,4096]{1,0:T(8,128)(2,1)S(1)}, u32[]{:S(2)}, u32[]{:S(2)}) %collective-permute-start) | collective-permute-done | bytes 4194336 | tf_op jit(solution)/shard_map/ppermute | solution.py:19
  108.2 1.9 collective-permute-done.1
  110.2 2.7 collective-permute-start.3
  112.9 86.1 %collective-permute-done.2 = bf16[512,4096]{1,0:T(8,128)(2,1)S(1)} collective-permute-done((bf16[512,4096]{1,0:T(8,128)(2,1)S(1)}, bf16[512,4096]{1,0:T(8,128)(2,1)S(1)}, u32[]{:S(2)}, u32[]{:S(2)}) %collective-permute-start.2) | collective-permute-done | bytes 4194336 | tf_op jit(solution)/shard_map/ppermute | solution.py:19
  199.0 1.9 collective-permute-done.3
  201.0 2.8 collective-permute-start.5
  203.8 86.5 %collective-permute-done.4 = bf16[512,4096]{1,0:T(8,128)(2,1)} collective-permute-done((bf16[512,4096]{1,0:T(8,128)(2,1)S(1)}, bf16[512,4096]{1,0:T(8,128)(2,1)}, u32[]{:S(2)}, u32[]{:S(2)}) %collective-permute-start.4) | collective-permute-done | bytes 4194336 | tf_op jit(solution)/shard_map/ppermute | solution.py:19
  290.3 5.0 %constant_dynamic-update-slice_fusion.6 = bf16[4096,4096]{1,0:T(8,128)(2,1)} fusion(bf16[4096,4096]{1,0:T(8,128)(2,1)} %get-tuple-element.2, bf16[512,4096]{1,0:T(8,128)(2,1)} %copy-done.3, s32[]{:T(128)S(6)} %select_n.64), kind=kLoop, calls=%fused_computation.11 | loop fusion | bytes 8388612 | tf_op jit(solution)/shard_map/dynamic_update_slice | solution.py:20
  295.3 2.2 constant_dynamic-update-slice_fusion.5
  297.6 2.2 constant_dynamic-update-slice_fusion.4
  299.8 4.7 %constant_dynamic-update-slice_fusion.3 = bf16[4096,4096]{1,0:T(8,128)(2,1)} fusion(bf16[4096,4096]{1,0:T(8,128)(2,1)} %constant_dynamic-update-slice_fusion.4, bf16[512,4096]{1,0:T(8,128)(2,1)} %collective-permute-done.3, s32[]{:T(128)S(6)} %select_n.70), kind=kLoop, calls=%fused_computation.8 | loop fusion | bytes 8388612 | tf_op jit(solution)/shard_map/dynamic_update_slice | solution.py:25
  304.4 4.7 %constant_dynamic-update-slice_fusion.2 = bf16[4096,4096]{1,0:T(8,128)(2,1)} fusion(bf16[4096,4096]{1,0:T(8,128)(2,1)} %constant_dynamic-update-slice_fusion.3, bf16[512,4096]{1,0:T(8,128)(2,1)} %collective-permute-done.4, s32[]{:T(128)S(6)} %select_n.72), kind=kLoop, calls=%fused_computation.7 | loop fusion | bytes 8388612 | tf_op jit(solution)/shard_map/dynamic_update_slice | solution.py:20
  309.1 4.8 %constant_dynamic-update-slice_fusion.1 = bf16[4096,4096]{1,0:T(8,128)(2,1)} fusion(bf16[4096,4096]{1,0:T(8,128)(2,1)} %constant_dynamic-update-slice_fusion.2, bf16[512,4096]{1,0:T(8,128)(2,1)} %collective-permute-done.5, s32[]{:T(128)S(6)} %select_n.74), kind=kLoop, calls=%fused_computation.6 | loop fusion | bytes 8388612 | tf_op jit(solution)/shard_map/dynamic_update_slice | solution.py:25
  313.9 25.6 %collective-permute-done.6 = bf16[512,4096]{1,0:T(8,128)(2,1)} collective-permute-done((bf16[512,4096]{1,0:T(8,128)(2,1)}, bf16[512,4096]{1,0:T(8,128)(2,1)}, u32[]{:S(2)}, u32[]{:S(2)}) %collective-permute-start.6) | collective-permute-done | bytes 4194336 | tf_op jit(solution)/shard_map/ppermute | solution.py:19
  339.4 4.6 %constant_dynamic-update-slice_fusion = bf16[4096,4096]{1,0:T(8,128)(2,1)} fusion(bf16[4096,4096]{1,0:T(8,128)(2,1)} %constant_dynamic-update-slice_fusion.1, bf16[512,4096]{1,0:T(8,128)(2,1)} %collective-permute-done.6, s32[]{:T(128)S(6)} %select_n.76), kind=kLoop, calls=%fused_computation.5 | loop fusion | bytes 8388612 | tf_op jit(solution)/shard_map/dynamic_update_slice | solution.py:20
  344.1 24.0 %convolution_convert_fusion.clone.4 = bf16[4096,512]{1,0:T(8,128)(2,1)} fusion(bf16[4096,4096]{1,0:T(8,128)(2,1)} %constant_dynamic-update-slice_fusion, bf16[512,4096]{1,0:T(8,128)(2,1)S(1)} %copy-done.2), kind=kOutput, calls=%fused_computation.2.clone.clone.clone.1 | convolution fusion | flops 17181966336 | bytes 41943040 | tf_op jit(solution)/shard_map/dot_general | solution.py:32
  368.1 28.3 %multiply_subtract_fusion = f32[512,4096]{1,0:T(8,128)} fusion(f32[512,4096]{1,0:T(8,128)} %param.1, bf16[4096,4096]{1,0:T(8,128)(2,1)} %constant_dynamic-update-slice_fusion, bf16[4096,512]{1,0:T(8,128)(2,1)} %convolution_convert_fusion.clone.4), kind=kOutput, calls=%fused_computation.1 | convolution fusion | flops 17186160640 | bytes 54525952 | tf_op jit(solution)/shard_map/dot_general | solution.py:32
  396.4 11.5 %copy.4 = f32[64,8,8,512]{3,2,1,0:T(8,128)S(1)} copy(f32[64,8,8,512]{3,1,2,0:T(8,128)} %bitcast.21) | data formatting | bytes 16777216
  409.1 4.5 %gather_fusion = f32[512]{0:T(512)S(1)} fusion(f32[512,512]{1,0:T(8,128)S(1)} %bitcast.20, s32[512]{0:T(512)S(1)} %bitcast.18), kind=kCustom, calls=%fused_computation | custom fusion | bytes 8192 | tf_op jit(solution)/shard_map/jit(diagonal)/cond/branch_0_fun/gather | solution.py:38
  414.2 17.1 %psum.7 = f32[]{:T(128)} all-reduce(f32[]{:T(128)} %reduce_sum.9), channel_id=1, replica_groups=mesh['ka'=4,'row'=8] {'row'}, use_global_device_ids=true, to_apply=%region_1.2 | all-reduce | flops 1 | bytes 8 | tf_op jit(solution)/shard_map/psum | solution.py:51
  (24 shorter events, 2.5 us)
Async XLA Ops:
  0.6 13.1 %copy-start = (f32[512,4096]{1,0:T(8,128)S(1)}, f32[512,4096]{1,0:T(8,128)}, u32[]{:S(2)}) copy-start(f32[512,4096]{1,0:T(8,128)} %param.1) | copy-start | bytes 25165828
  16.7 2.1 copy-start.1
  16.7 91.5 %collective-permute-start = (bf16[512,4096]{1,0:T(8,128)(2,1)S(1)}, bf16[512,4096]{1,0:T(8,128)(2,1)S(1)}, u32[]{:S(2)}, u32[]{:S(2)}) collective-permute-start(bf16[512,4096]{1,0:T(8,128)(2,1)S(1)} %get-tuple-element.3), channel_id=1, source_target_pairs={{0,1},{1,2},{2,3},{3,4},{4,5},{5,6},{6,7},{7,0},{8,9},{9,10},{10,1... | collective-permute-start | bytes 12582920 | tf_op jit(solution)/shard_map/ppermute | solution.py:19
  18.8 91.3 %collective-permute-start.1 = (bf16[512,4096]{1,0:T(8,128)(2,1)S(1)}, bf16[512,4096]{1,0:T(8,128)(2,1)S(1)}, u32[]{:S(2)}, u32[]{:S(2)}) collective-permute-start(bf16[512,4096]{1,0:T(8,128)(2,1)S(1)} %get-tuple-element.3), channel_id=1, source_target_pairs={{0,7},{1,0},{2,1},{3,2},{4,3},{5,4},{6,5},{7,6},{8,15},{9,8},{10,9... | collective-permute-start | bytes 12582920 | tf_op jit(solution)/shard_map/ppermute | solution.py:24
  108.2 2.0 copy-start.3
  108.2 90.8 %collective-permute-start.2 = (bf16[512,4096]{1,0:T(8,128)(2,1)S(1)}, bf16[512,4096]{1,0:T(8,128)(2,1)S(1)}, u32[]{:S(2)}, u32[]{:S(2)}) collective-permute-start(bf16[512,4096]{1,0:T(8,128)(2,1)S(1)} %collective-permute-done), channel_id=1, source_target_pairs={{0,1},{1,2},{2,3},{3,4},{4,5},{5,6},{6,7},{7,0},{8,9},{9,10},{10,1... | collective-permute-start | bytes 12582920 | tf_op jit(solution)/shard_map/ppermute | solution.py:19
  110.2 88.8 %copy-start.4 = (bf16[512,4096]{1,0:T(8,128)(2,1)}, bf16[512,4096]{1,0:T(8,128)(2,1)S(1)}, u32[]{:S(2)}) copy-start(bf16[512,4096]{1,0:T(8,128)(2,1)S(1)} %collective-permute-done.1) | copy-start | bytes 12582916
  110.2 90.6 %collective-permute-start.3 = (bf16[512,4096]{1,0:T(8,128)(2,1)S(1)}, bf16[512,4096]{1,0:T(8,128)(2,1)}, u32[]{:S(2)}, u32[]{:S(2)}) collective-permute-start(bf16[512,4096]{1,0:T(8,128)(2,1)S(1)} %collective-permute-done.1), channel_id=1, source_target_pairs={{0,7},{1,0},{2,1},{3,2},{4,3},{5,4},{6,5},{7,6},{8,15},{9,8},{10,9... | collective-permute-start | bytes 12582920 | tf_op jit(solution)/shard_map/ppermute | solution.py:24
  199.0 2.0 copy-start.6
  199.0 91.3 %collective-permute-start.4 = (bf16[512,4096]{1,0:T(8,128)(2,1)S(1)}, bf16[512,4096]{1,0:T(8,128)(2,1)}, u32[]{:S(2)}, u32[]{:S(2)}) collective-permute-start(bf16[512,4096]{1,0:T(8,128)(2,1)S(1)} %collective-permute-done.2), channel_id=1, source_target_pairs={{0,1},{1,2},{2,3},{3,4},{4,5},{5,6},{6,7},{7,0},{8,9},{9,10},{10,1... | collective-permute-start | bytes 12582920 | tf_op jit(solution)/shard_map/ppermute | solution.py:19
  201.0 108.1 %collective-permute-start.5 = (bf16[512,4096]{1,0:T(8,128)(2,1)}, bf16[512,4096]{1,0:T(8,128)(2,1)}, u32[]{:S(2)}, u32[]{:S(2)}) collective-permute-start(bf16[512,4096]{1,0:T(8,128)(2,1)} %collective-permute-done.3), channel_id=1, source_target_pairs={{0,7},{1,0},{2,1},{3,2},{4,3},{5,4},{6,5},{7,6},{8,15},{9,8},{10,9... | collective-permute-start | bytes 12582920 | tf_op jit(solution)/shard_map/ppermute | solution.py:24
  290.3 49.1 %collective-permute-start.6 = (bf16[512,4096]{1,0:T(8,128)(2,1)}, bf16[512,4096]{1,0:T(8,128)(2,1)}, u32[]{:S(2)}, u32[]{:S(2)}) collective-permute-start(bf16[512,4096]{1,0:T(8,128)(2,1)} %collective-permute-done.4), channel_id=1, source_target_pairs={{0,1},{1,2},{2,3},{3,4},{4,5},{5,6},{6,7},{7,0},{8,9},{9,10},{10,1... | collective-permute-start | bytes 12582920 | tf_op jit(solution)/shard_map/ppermute | solution.py:19
  290.3 5.0 %copy-start.5 = (bf16[512,4096]{1,0:T(8,128)(2,1)S(1)}, bf16[512,4096]{1,0:T(8,128)(2,1)}, u32[]{:S(2)}) copy-start(bf16[512,4096]{1,0:T(8,128)(2,1)} %copy-done.4) | copy-start | bytes 12582916
  290.3 7.2 %copy-start.7 = (bf16[512,4096]{1,0:T(8,128)(2,1)S(1)}, bf16[512,4096]{1,0:T(8,128)(2,1)}, u32[]{:S(2)}) copy-start(bf16[512,4096]{1,0:T(8,128)(2,1)} %copy-done.6) | copy-start | bytes 12582916
  309.1 35.0 %copy-start.2 = (bf16[512,4096]{1,0:T(8,128)(2,1)S(1)}, bf16[512,4096]{1,0:T(8,128)(2,1)}, u32[]{:S(2)}) copy-start(bf16[512,4096]{1,0:T(8,128)(2,1)} %copy-done.1) | copy-start | bytes 12582916
